TPU v7x, 32 devices: a whole 2x2x4 slice. The times are simulated.
32 devices in a mesh: leaf: 8 (over z, x), rows: 4 (over y, core).
Axes of the slice: x: 2, y: 2, z: 4, core: 2. Of those that a mesh axis runs over, the one named last changes fastest.
Arguments:
- right_side: float32 [8, 32768], P(None, ('leaf', 'rows')), may hold values from -6 to 6
- diagonal: float32 [32768], P(('leaf', 'rows')), may hold values from 0.5 to 4
- tree_order: int32 [32768], P(('leaf', 'rows')), may hold values from 0 to 32767, as said below
- mid_perm: int32 [8], replicated, may hold values from 0 to 7, each once
- col_factor: bfloat16 [32768, 384], P(('leaf', 'rows')), may hold values from -0.1875 to 0.1875
- mid_factor: bfloat16 [3072, 768], P('leaf', 'rows'), may hold values from -0.15625 to 0.15625
- pre_factor: bfloat16 [3072, 768], P('leaf', 'rows'), may hold values from -0.15625 to 0.15625
- row_factor: bfloat16 [48, 32768], P(None, ('leaf', 'rows')), may hold values from -0.875 to 0.875
Outputs:
- solution: float32 [8, 32768], P(None, ('leaf', 'rows'))
- residual: float32 [8, 32768], P(None, ('leaf', 'rows'))
Inputs may be any that keep to these rules, and one draw needn't show every extreme that they name: `tree_order`: each aligned run of 1024 entries, the run starting at b * 1024, is a permutation of b * 1024 to (b + 1) * 1024 - 1. `mid_perm`: a permutation of 0 to 7.
All inputs are finite; a program needn't handle non-finite values.
Results may differ from a plain program's by a relative error of at most 0.025.
Values may be sent and summed in bfloat16 or wider, within the bound.
No kernel may reach another device: no remote copies, remote signals or barrier semaphores. Data moves between devices by JAX's collectives and lax.ppermute only.
A program may use at most 64 MiB of HBM per device.

v0:
```python
import jax
import jax.numpy as jnp
from jax import lax
from jax.sharding import PartitionSpec as P

ITERS = 2


def curvature(first, second):
    return lax.psum(jnp.sum(first * second, axis=1), ("leaf", "rows"))


def precond_norm(first, second):
    return lax.psum(jnp.sum(first * second, axis=1), ("leaf", "rows"))


def per_device(
    right_side, diagonal, tree_order, mid_perm, col_factor, mid_factor, pre_factor, row_factor
):
    sides, points = right_side.shape
    rank_size = row_factor.shape[0]
    leaves = mid_perm.shape[0]
    row_count = mid_factor.shape[1] // rank_size
    local_index = tree_order % points
    slot_ids = jnp.arange(leaves, dtype=jnp.int32)
    onehot = (mid_perm[:, None] == slot_ids[None, :]).astype(jnp.bfloat16)
    col_split = col_factor.reshape(points, leaves, rank_size)
    own_gram = jnp.dot(row_factor, row_factor.T, preferred_element_type=jnp.float32)
    gram_blocks = lax.all_gather(own_gram[None], "rows", axis=0, tiled=True)

    def gram_apply(field, mid_weight):
        taken_tree = jnp.take(field, local_index, axis=1).astype(jnp.bfloat16)
        coeffs = jnp.einsum(
            "sn,ngk->gsk", taken_tree, col_split, preferred_element_type=jnp.float32
        ).astype(jnp.bfloat16)
        outgoing = jnp.einsum(
            "qg,gsk->qsk", onehot, coeffs, preferred_element_type=jnp.float32
        ).astype(jnp.bfloat16)
        incoming = lax.all_to_all(
            outgoing.reshape(leaves, sides * rank_size),
            "leaf",
            split_axis=0,
            concat_axis=0,
            tiled=True,
        )
        incoming = incoming.reshape(leaves, sides, rank_size)
        weight_split = mid_weight.reshape(leaves, rank_size, row_count * rank_size)
        partial_value = jnp.einsum(
            "lsk,lkm->sm", incoming, weight_split, preferred_element_type=jnp.float32
        )
        totals = lax.psum(partial_value, "rows")
        head_coef = lax.optimization_barrier(totals.astype(jnp.bfloat16)).astype(jnp.float32)
        head_coef = head_coef.reshape(sides, row_count, rank_size)
        gathered = jnp.einsum(
            "sjk,jkm->sjm", head_coef, gram_blocks, precision=lax.Precision.HIGHEST
        )
        gathered = gathered.reshape(sides, row_count * rank_size).astype(jnp.bfloat16)
        returned = jnp.einsum(
            "sm,lkm->lsk", gathered, weight_split, preferred_element_type=jnp.float32
        ).astype(jnp.bfloat16)
        arrived = lax.all_to_all(
            returned.reshape(leaves, sides * rank_size),
            "leaf",
            split_axis=0,
            concat_axis=0,
            tiled=True,
        )
        arrived = arrived.reshape(leaves, sides, rank_size)
        unsent = jnp.einsum(
            "qg,qsk->gsk", onehot, arrived, preferred_element_type=jnp.float32
        ).astype(jnp.bfloat16)
        tree_out = jnp.einsum("gsk,ngk->sn", unsent, col_split, preferred_element_type=jnp.float32)
        return jnp.zeros_like(tree_out).at[:, local_index].set(tree_out)

    def apply_precond(field):
        return field / diagonal[None, :] + gram_apply(field, pre_factor)

    solution = jnp.zeros_like(right_side)
    residual = right_side
    precond = apply_precond(residual)
    direction = precond
    precond_dot = precond_norm(residual, precond)
    for iteration in range(ITERS):
        image = diagonal[None, :] * direction + gram_apply(direction, mid_factor)
        alpha_step = precond_dot / curvature(direction, image)
        solution = solution + alpha_step[:, None] * direction
        residual = residual - alpha_step[:, None] * image
        if iteration + 1 < ITERS:
            precond = apply_precond(residual)
            dot_next = precond_norm(residual, precond)
            direction = precond + (dot_next / precond_dot)[:, None] * direction
            precond_dot = dot_next
    return (solution, residual)


def solution(mesh):
    return jax.shard_map(
        per_device,
        mesh=mesh,
        in_specs=(
            P(None, ("leaf", "rows")),
            P(("leaf", "rows")),
            P(("leaf", "rows")),
            P(),
            P(("leaf", "rows"), None),
            P("leaf", "rows"),
            P("leaf", "rows"),
            P(None, ("leaf", "rows")),
        ),
        out_specs=(P(None, ("leaf", "rows")), P(None, ("leaf", "rows"))),
        check_vma=False,
    )
```

profile of v0, /device:TPU:0, one launch (start us, length us, event | category | flops | bytes accessed | tf_op | source)
XLA Modules:
  0.0 275.6 jit_solution(600486382952462527)
XLA Ops:
  0.6 0.7 compare_and_fusion
  1.4 0.9 copy.167
  2.3 3.2 %gather_fusion = bf16[1024,8]{1,0:T(8,128)(2,1)S(1)} fusion(bf16[8,1024]{0,1:T(8,128)(2,1)S(1)} %copy.167, s32[1024]{0:T(1024)S(1)} %broadcast_clamp_fusion), kind=kCustom, calls=%fused_computation.clone | custom fusion | bytes 36864 | tf_op jit(solution)/shard_map/jit(_take)/gather | solution.py:32
  5.6 1.4 copy.169
  7.1 0.5 fusion
  8.0 0.5 broadcast.102
  8.5 0.7 reduce.8
  9.2 0.7 reshape.246
  9.9 7.3 %all-to-all-start = ((bf16[8,2,192]{2,1,0:T(2,128)(2,1)}), bf16[8,2,192]{2,1,0:T(2,128)(2,1)S(1)}, u32[]{:S(2)}, u32[]{:S(2)}) async-start(bf16[8,2,192]{2,1,0:T(2,128)(2,1)} %reshape.246), calls=%async_computation | async-start | bytes 16384 | tf_op jit(solution)/shard_map/all_to_all | solution.py:39
  17.5 5.3 %all-gather = f32[192,48]{1,0:T(8,128)S(1)} all-gather(f32[48,48]{1,0:T(8,128)S(1)} %fusion.74), channel_id=2, replica_groups=mesh['leaf'=8,'rows'=4] {'rows'}, dimensions={0}, use_global_device_ids=true | all-gather | bytes 46080 | tf_op jit(solution)/shard_map/all_gather | solution.py:29
  22.8 0.9 all-to-all-done
  24.1 6.3 %psum.56 = bf16[8,192]{1,0:T(8,128)(2,1)S(1)} all-reduce(f32[8,192]{1,0:T(8,128)S(1)} %convolution_bitcast_fusion.7), channel_id=1, replica_groups=mesh['leaf'=8,'rows'=4] {'rows'}, use_global_device_ids=true, to_apply=%region_0.2 | all-reduce | flops 1536 | bytes 9216 | tf_op jit(solution)/shard_map/psum | solution.py:51
  31.1 0.7 reduce.9
  31.9 12.3 %all_to_all.80 = bf16[8,2,192]{2,1,0:T(2,128)(2,1)S(1)} all-to-all(bf16[8,2,192]{2,1,0:T(2,128)(2,1)S(1)} %reshape.248), channel_id=1, replica_groups=mesh['leaf'=8,'rows'=4] {'leaf'}, dimensions={0} | all-to-all | bytes 12288 | tf_op jit(solution)/shard_map/all_to_all | solution.py:61
  44.5 0.3 convolution_bitcast_fusion.3
  45.0 3.2 %scatter_custom_fusion = f32[8,1024]{0,1:T(8,128)S(1)} fusion(s32[1024]{0:T(1024)S(1)} %get-tuple-element.16, f32[1024,8]{1,0:T(8,128)S(1)} %copy.180, f32[]{:T(128)} %constant.15.clone.1), kind=kCustom, calls=%fused_computation.54 | custom fusion | bytes 32772 | tf_op jit(solution)/shard_map/scatter | solution.py:73
  48.4 0.6 copy-done.1
  49.2 3.2 %gather_fusion.1 = bf16[1024,8]{1,0:T(8,128)(2,1)S(1)} fusion(bf16[8,1024]{0,1:T(8,128)(2,1)S(1)} %copy.182, s32[1024]{0:T(1024)S(1)} %broadcast_clamp_fusion), kind=kCustom, calls=%fused_computation.1.clone | custom fusion | bytes 36864 | tf_op jit(solution)/shard_map/jit(_take)/gather | solution.py:32
  52.5 0.5 fusion.2
  53.3 0.7 reduce.10
  54.0 0.7 reshape.250
  54.7 3.3 %all-to-all-start.2 = ((bf16[8,2,192]{2,1,0:T(2,128)(2,1)}), bf16[8,2,192]{2,1,0:T(2,128)(2,1)S(1)}, u32[]{:S(2)}, u32[]{:S(2)}) async-start(bf16[8,2,192]{2,1,0:T(2,128)(2,1)} %reshape.250), calls=%async_computation.2 | async-start | bytes 16384 | tf_op jit(solution)/shard_map/all_to_all | solution.py:39
  58.2 6.3 %all-to-all-done.2 = bf16[8,2,192]{2,1,0:T(2,128)(2,1)S(1)} async-done(((bf16[8,2,192]{2,1,0:T(2,128)(2,1)}), bf16[8,2,192]{2,1,0:T(2,128)(2,1)S(1)}, u32[]{:S(2)}, u32[]{:S(2)}) %all-to-all-start.2) | async-done | bytes 6176 | tf_op jit(solution)/shard_map/all_to_all | solution.py:39
  64.9 6.0 %psum.58 = bf16[8,192]{1,0:T(8,128)(2,1)S(1)} all-reduce(f32[8,192]{1,0:T(8,128)S(1)} %convolution_bitcast_fusion.6), channel_id=1, replica_groups=mesh['leaf'=8,'rows'=4] {'rows'}, use_global_device_ids=true, to_apply=%region_4.6 | all-reduce | flops 1536 | bytes 9216 | tf_op jit(solution)/shard_map/psum | solution.py:51
  71.6 0.7 reduce.11
  72.3 8.9 %all_to_all.81 = bf16[8,2,192]{2,1,0:T(2,128)(2,1)S(1)} all-to-all(bf16[8,2,192]{2,1,0:T(2,128)(2,1)S(1)} %reshape.252), channel_id=1, replica_groups=mesh['leaf'=8,'rows'=4] {'leaf'}, dimensions={0} | all-to-all | bytes 12288 | tf_op jit(solution)/shard_map/all_to_all | solution.py:61
  81.6 0.3 convolution_bitcast_fusion.2
  82.0 3.2 %scatter_custom_fusion.1 = f32[8,1024]{0,1:T(8,128)S(1)} fusion(s32[1024]{0:T(1024)S(1)} %get-tuple-element.16, f32[1024,8]{1,0:T(8,128)S(1)} %copy.194, f32[]{:T(128)} %constant.15.clone.1), kind=kCustom, calls=%fused_computation.52 | custom fusion | bytes 32772 | tf_op jit(solution)/shard_map/scatter | solution.py:73
  85.6 38.2 %all-reduce = (f32[8]{0:T(128)S(1)}, f32[8]{0:T(128)S(1)}) all-reduce(f32[8]{0:T(128)S(1)} %get-tuple-element.12, f32[8]{0:T(128)S(1)} %get-tuple-element.11), channel_id=1, replica_groups=mesh['leaf'=8,'rows'=4] {'leaf','rows'}, use_global_device_ids=true, to_apply=%region_3.5 | all-reduce | flops 16 | bytes 128 | tf_op jit(solution)/shard_map/psum | solution.py:14
  124.1 3.2 %gather_fusion.2 = bf16[1024,8]{1,0:T(8,128)(2,1)S(1)} fusion(bf16[8,1024]{0,1:T(8,128)(2,1)S(1)} %copy.196, s32[1024]{0:T(1024)S(1)} %broadcast_clamp_fusion), kind=kCustom, calls=%fused_computation.2.clone | custom fusion | bytes 36864 | tf_op jit(solution)/shard_map/jit(_take)/gather | solution.py:32
  127.4 0.5 fusion.4
  128.2 0.7 reduce.12
  129.0 11.0 %all_to_all.82 = bf16[8,2,192]{2,1,0:T(2,128)(2,1)S(1)} all-to-all(bf16[8,2,192]{2,1,0:T(2,128)(2,1)S(1)} %reshape.254), channel_id=1, replica_groups=mesh['leaf'=8,'rows'=4] {'leaf'}, dimensions={0} | all-to-all | bytes 12288 | tf_op jit(solution)/shard_map/all_to_all | solution.py:39
  140.3 6.1 %psum.60 = bf16[8,192]{1,0:T(8,128)(2,1)S(1)} all-reduce(f32[8,192]{1,0:T(8,128)S(1)} %convolution_bitcast_fusion.5), channel_id=1, replica_groups=mesh['leaf'=8,'rows'=4] {'rows'}, use_global_device_ids=true, to_apply=%region_8.10 | all-reduce | flops 1536 | bytes 9216 | tf_op jit(solution)/shard_map/psum | solution.py:51
  147.1 0.7 reduce.13
  147.9 8.9 %all_to_all.83 = bf16[8,2,192]{2,1,0:T(2,128)(2,1)S(1)} all-to-all(bf16[8,2,192]{2,1,0:T(2,128)(2,1)S(1)} %reshape.256), channel_id=1, replica_groups=mesh['leaf'=8,'rows'=4] {'leaf'}, dimensions={0} | all-to-all | bytes 12288 | tf_op jit(solution)/shard_map/all_to_all | solution.py:61
  157.6 3.4 %scatter_custom_fusion.2 = f32[8,1024]{0,1:T(8,128)S(1)} fusion(s32[1024]{0:T(1024)S(1)} %get-tuple-element.16, f32[1024,8]{1,0:T(8,128)S(1)} %copy.207, f32[]{:T(128)} %constant.15.clone.1), kind=kCustom, calls=%fused_computation.50 | custom fusion | bytes 32772 | tf_op jit(solution)/shard_map/scatter | solution.py:73
  161.3 38.2 %psum.61 = f32[8]{0:T(128)S(1)} all-reduce(f32[8]{0:T(128)S(1)} %multiply_reduce_fusion.1), channel_id=1, replica_groups=mesh['leaf'=8,'rows'=4] {'leaf','rows'}, use_global_device_ids=true, to_apply=%region_11.13 | all-reduce | flops 8 | bytes 64 | tf_op jit(solution)/shard_map/psum | solution.py:14
  199.7 3.2 %gather_fusion.3 = bf16[1024,8]{1,0:T(8,128)(2,1)S(1)} fusion(bf16[8,1024]{0,1:T(8,128)(2,1)S(1)} %copy.209, s32[1024]{0:T(1024)S(1)} %broadcast_clamp_fusion), kind=kCustom, calls=%fused_computation.3.clone | custom fusion | bytes 36864 | tf_op jit(solution)/shard_map/jit(_take)/gather | solution.py:32
  203.0 0.5 fusion.6
  203.8 0.7 reduce.14
  204.6 11.0 %all_to_all.84 = bf16[8,2,192]{2,1,0:T(2,128)(2,1)S(1)} all-to-all(bf16[8,2,192]{2,1,0:T(2,128)(2,1)S(1)} %reshape.258), channel_id=1, replica_groups=mesh['leaf'=8,'rows'=4] {'leaf'}, dimensions={0} | all-to-all | bytes 12288 | tf_op jit(solution)/shard_map/all_to_all | solution.py:39
  216.0 6.1 %psum.62 = bf16[8,192]{1,0:T(8,128)(2,1)S(1)} all-reduce(f32[8,192]{1,0:T(8,128)S(1)} %convolution_bitcast_fusion.4), channel_id=1, replica_groups=mesh['leaf'=8,'rows'=4] {'rows'}, use_global_device_ids=true, to_apply=%region_12.14 | all-reduce | flops 1536 | bytes 9216 | tf_op jit(solution)/shard_map/psum | solution.py:51
  222.7 0.7 reduce.15
  223.5 8.9 %all_to_all.85 = bf16[8,2,192]{2,1,0:T(2,128)(2,1)S(1)} all-to-all(bf16[8,2,192]{2,1,0:T(2,128)(2,1)S(1)} %reshape.260), channel_id=1, replica_groups=mesh['leaf'=8,'rows'=4] {'leaf'}, dimensions={0} | all-to-all | bytes 12288 | tf_op jit(solution)/shard_map/all_to_all | solution.py:61
  233.2 3.2 %scatter_custom_fusion.3 = f32[8,1024]{0,1:T(8,128)S(1)} fusion(s32[1024]{0:T(1024)S(1)} %get-tuple-element.16, f32[1024,8]{1,0:T(8,128)S(1)} %copy.220, f32[]{:T(128)} %constant.15.clone.1), kind=kCustom, calls=%fused_computation.48 | custom fusion | bytes 32772 | tf_op jit(solution)/shard_map/scatter | solution.py:73
  236.7 38.2 %psum.63 = f32[8]{0:T(128)S(1)} all-reduce(f32[8]{0:T(128)S(1)} %multiply_reduce_fusion), channel_id=1, replica_groups=mesh['leaf'=8,'rows'=4] {'leaf','rows'}, use_global_device_ids=true, to_apply=%region_15.17 | all-reduce | flops 8 | bytes 64 | tf_op jit(solution)/shard_map/psum | solution.py:10
  274.9 0.7 multiply_subtract_fusion
  (115 shorter events, 11.5 us)
Async XLA Ops:
  0.6 16.6 %copy-start = (bf16[48,1024]{1,0:T(8,128)(2,1)S(1)}, bf16[48,1024]{1,0:T(8,128)(2,1)}, u32[]{:S(2)}) copy-start(bf16[48,1024]{1,0:T(8,128)(2,1)} %param.17) | copy-start | bytes 294916
  7.1 0.7 copy-start.5
  7.9 9.4 %copy-start.3 = (bf16[384,192]{0,1:T(8,128)(2,1)S(1)}, bf16[384,192]{0,1:T(8,128)(2,1)}, u32[]{:S(2)}) copy-start(bf16[384,192]{0,1:T(8,128)(2,1)} %param.16) | copy-start | bytes 442372
  9.9 13.8 %all-to-all-start = ((bf16[8,2,192]{2,1,0:T(2,128)(2,1)}), bf16[8,2,192]{2,1,0:T(2,128)(2,1)S(1)}, u32[]{:S(2)}, u32[]{:S(2)}) async-start(bf16[8,2,192]{2,1,0:T(2,128)(2,1)} %reshape.246), calls=%async_computation | async-start | bytes 16384 | tf_op jit(solution)/shard_map/all_to_all | solution.py:39
  48.3 0.8 copy-start.1
  48.3 0.8 copy-start.2
  52.5 5.5 %copy-start.4 = (bf16[384,192]{0,1:T(8,128)(2,1)S(1)}, bf16[384,192]{0,1:T(8,128)(2,1)}, u32[]{:S(2)}) copy-start(bf16[384,192]{0,1:T(8,128)(2,1)} %param.15) | copy-start | bytes 442372
  54.7 9.8 %all-to-all-start.2 = ((bf16[8,2,192]{2,1,0:T(2,128)(2,1)}), bf16[8,2,192]{2,1,0:T(2,128)(2,1)S(1)}, u32[]{:S(2)}, u32[]{:S(2)}) async-start(bf16[8,2,192]{2,1,0:T(2,128)(2,1)} %reshape.250), calls=%async_computation.2 | async-start | bytes 16384 | tf_op jit(solution)/shard_map/all_to_all | solution.py:39
where the time goes:
time: 277 us; the launch traced here: 276 us
  blocking collectives  205 us (74%)
  local copies, waits for them, and re-layouts  37.2 us (13%)
  starting transfers between devices  10.6 us (4%)
  other arithmetic  7.88 us (3%)
  waiting for transfers between devices  7.17 us (3%)
  matrix products  6.49 us (2%)
    psum x2, blocking collectives, precond_norm(): return lax.psum(jnp.sum(first * second, axis=1), ('leaf', 'rows'))  76.4 us
    all_to_all x4, blocking collectives, gram_apply(): lax.all_to_all(returned.reshape(leaves, sides * rank_size), 'leaf', split...  38.9 us
    psum x1, blocking collectives, curvature(): return lax.psum(jnp.sum(first * second, axis=1), ('leaf', 'rows'))  38.2 us
    psum x4, blocking collectives, gram_apply(): totals = lax.psum(partial_value, 'rows')  24.5 us
    all_to_all x2, blocking collectives, gram_apply(): lax.all_to_all(outgoing.reshape(leaves, sides * rank_size), 'leaf', split...  21.9 us
    scatter x8, local copies, waits for them, and re-layouts, gram_apply(): return jnp.zeros_like(tree_out).at[:, local_index].set(tree_out)  13.7 us
    gather x8, local copies, waits for them, and re-layouts, gram_apply(): taken_tree = jnp.take(field, local_index, axis=1).astype(jnp.bfloat16)  13.3 us
    all_to_all x2, starting transfers between devices, gram_apply(): lax.all_to_all(outgoing.reshape(leaves, sides * rank_size), 'leaf', split...  10.6 us
  transfers between devices with their start and end apart: 2, of which 2 were waited for; matrix products, arithmetic and copies ran while one was open for 0% of the time, Pallas kernels for 0%

commit v1 on v0

--- a/solution.py
+++ b/solution.py
@@ -6,12 +6,17 @@
 ITERS = 2
 
 
+def teams_bind(row_data):
+    frame_out = jax.lax.psum(row_data, "rows")
+    return jax.lax.psum(frame_out, "leaf")
+
+
 def curvature(first, second):
     return lax.psum(jnp.sum(first * second, axis=1), ("leaf", "rows"))
 
 
 def precond_norm(first, second):
-    return lax.psum(jnp.sum(first * second, axis=1), ("leaf", "rows"))
+    return teams_bind(jnp.sum(first * second, axis=1))
 
 
 def per_device(

time: 277 us -> 284 us (1.025)
  blocking collectives: 205 us -> 212 us
    psum x1 -> x2, blocking collectives: 38.2 us -> 76.4 us  [curvature(): return lax.psum(jnp.sum(first * second, axis=1), ('leaf', 'rows'))]
    psum x2 -> x4, blocking collectives: 76.4 us -> 49.6 us  [the longest x2 38.1 us: teams_bind(): return jax.lax.psum(frame_out, 'leaf')]
    all_to_all x2, blocking collectives: 21.9 us -> 17.9 us  [gram_apply(): lax.all_to_all(outgoing.reshape(leaves, sides * rank_size), 'leaf', split...]
where the time goes in v1:
time: 284 us; the launch traced here: 283 us
  blocking collectives  212 us (75%)
  local copies, waits for them, and re-layouts  37 us (13%)
  starting transfers between devices  10.6 us (4%)
  other arithmetic  7.89 us (3%)
  waiting for transfers between devices  7.17 us (3%)
  matrix products  6.49 us (2%)
    psum x2, blocking collectives, curvature(): return lax.psum(jnp.sum(first * second, axis=1), ('leaf', 'rows'))  76.4 us
    all_to_all x4, blocking collectives, gram_apply(): lax.all_to_all(returned.reshape(leaves, sides * rank_size), 'leaf', split...  38.9 us
    psum x2, blocking collectives, teams_bind(): return jax.lax.psum(frame_out, 'leaf')  38.1 us
    psum x4, blocking collectives, gram_apply(): totals = lax.psum(partial_value, 'rows')  24.3 us
    all_to_all x2, blocking collectives, gram_apply(): lax.all_to_all(outgoing.reshape(leaves, sides * rank_size), 'leaf', split...  17.9 us
    scatter x8, local copies, waits for them, and re-layouts, gram_apply(): return jnp.zeros_like(tree_out).at[:, local_index].set(tree_out)  13.5 us
    gather x8, local copies, waits for them, and re-layouts, gram_apply(): taken_tree = jnp.take(field, local_index, axis=1).astype(jnp.bfloat16)  13.3 us
    psum x2, blocking collectives, teams_bind(): frame_out = jax.lax.psum(row_data, 'rows')  11.5 us
  transfers between devices with their start and end apart: 2, of which 2 were waited for; matrix products, arithmetic and copies ran while one was open for 0% of the time, Pallas kernels for 0%

profile of v1, /device:TPU:0, one launch (start us, length us, event | category | flops | bytes accessed | tf_op | source)
XLA Modules:
  0.0 282.6 jit_solution(3488124847591782563)
XLA Ops:
  0.6 0.7 compare_and_fusion
  1.4 0.9 copy.167
  2.3 3.2 %gather_fusion = bf16[1024,8]{1,0:T(8,128)(2,1)S(1)} fusion(bf16[8,1024]{0,1:T(8,128)(2,1)S(1)} %copy.167, s32[1024]{0:T(1024)S(1)} %broadcast_clamp_fusion), kind=kCustom, calls=%fused_computation.clone | custom fusion | bytes 36864 | tf_op jit(solution)/shard_map/jit(_take)/gather | solution.py:37
  5.6 1.4 copy.169
  8.0 0.5 broadcast.102
  8.5 0.7 reduce.8
  9.2 0.7 reshape.246
  9.9 7.3 %all-to-all-start = ((bf16[8,2,192]{2,1,0:T(2,128)(2,1)}), bf16[8,2,192]{2,1,0:T(2,128)(2,1)S(1)}, u32[]{:S(2)}, u32[]{:S(2)}) async-start(bf16[8,2,192]{2,1,0:T(2,128)(2,1)} %reshape.246), calls=%async_computation | async-start | bytes 16384 | tf_op jit(solution)/shard_map/all_to_all | solution.py:44
  17.5 5.3 %all-gather = f32[192,48]{1,0:T(8,128)S(1)} all-gather(f32[48,48]{1,0:T(8,128)S(1)} %fusion.74), channel_id=2, replica_groups=mesh['leaf'=8,'rows'=4] {'rows'}, dimensions={0}, use_global_device_ids=true | all-gather | bytes 46080 | tf_op jit(solution)/shard_map/all_gather | solution.py:34
  22.8 0.9 all-to-all-done
  24.1 6.3 %psum.70 = bf16[8,192]{1,0:T(8,128)(2,1)S(1)} all-reduce(f32[8,192]{1,0:T(8,128)S(1)} %convolution_bitcast_fusion.7), channel_id=1, replica_groups=mesh['leaf'=8,'rows'=4] {'rows'}, use_global_device_ids=true, to_apply=%region_0.2 | all-reduce | flops 1536 | bytes 9216 | tf_op jit(solution)/shard_map/psum | solution.py:56
  31.1 0.7 reduce.9
  31.9 12.3 %all_to_all.80 = bf16[8,2,192]{2,1,0:T(2,128)(2,1)S(1)} all-to-all(bf16[8,2,192]{2,1,0:T(2,128)(2,1)S(1)} %reshape.248), channel_id=1, replica_groups=mesh['leaf'=8,'rows'=4] {'leaf'}, dimensions={0} | all-to-all | bytes 12288 | tf_op jit(solution)/shard_map/all_to_all | solution.py:66
  45.0 3.2 %scatter_custom_fusion = f32[8,1024]{0,1:T(8,128)S(1)} fusion(s32[1024]{0:T(1024)S(1)} %get-tuple-element.14, f32[1024,8]{1,0:T(8,128)S(1)} %copy.180, f32[]{:T(128)} %constant.15.clone.1), kind=kCustom, calls=%fused_computation.54 | custom fusion | bytes 32772 | tf_op jit(solution)/shard_map/scatter | solution.py:78
  48.4 0.6 copy-done.1
  49.2 3.2 %gather_fusion.1 = bf16[1024,8]{1,0:T(8,128)(2,1)S(1)} fusion(bf16[8,1024]{0,1:T(8,128)(2,1)S(1)} %copy.182, s32[1024]{0:T(1024)S(1)} %broadcast_clamp_fusion), kind=kCustom, calls=%fused_computation.1.clone | custom fusion | bytes 36864 | tf_op jit(solution)/shard_map/jit(_take)/gather | solution.py:37
  52.5 0.5 fusion.2
  53.3 0.7 reduce.10
  54.0 0.7 reshape.250
  54.7 3.3 %all-to-all-start.2 = ((bf16[8,2,192]{2,1,0:T(2,128)(2,1)}), bf16[8,2,192]{2,1,0:T(2,128)(2,1)S(1)}, u32[]{:S(2)}, u32[]{:S(2)}) async-start(bf16[8,2,192]{2,1,0:T(2,128)(2,1)} %reshape.250), calls=%async_computation.2 | async-start | bytes 16384 | tf_op jit(solution)/shard_map/all_to_all | solution.py:44
  58.2 6.3 %all-to-all-done.2 = bf16[8,2,192]{2,1,0:T(2,128)(2,1)S(1)} async-done(((bf16[8,2,192]{2,1,0:T(2,128)(2,1)}), bf16[8,2,192]{2,1,0:T(2,128)(2,1)S(1)}, u32[]{:S(2)}, u32[]{:S(2)}) %all-to-all-start.2) | async-done | bytes 6176 | tf_op jit(solution)/shard_map/all_to_all | solution.py:44
  64.9 6.0 %psum.73 = bf16[8,192]{1,0:T(8,128)(2,1)S(1)} all-reduce(f32[8,192]{1,0:T(8,128)S(1)} %convolution_bitcast_fusion.6), channel_id=1, replica_groups=mesh['leaf'=8,'rows'=4] {'rows'}, use_global_device_ids=true, to_apply=%region_5.7 | all-reduce | flops 1536 | bytes 9216 | tf_op jit(solution)/shard_map/psum | solution.py:56
  71.6 0.7 reduce.11
  72.3 8.9 %all_to_all.81 = bf16[8,2,192]{2,1,0:T(2,128)(2,1)S(1)} all-to-all(bf16[8,2,192]{2,1,0:T(2,128)(2,1)S(1)} %reshape.252), channel_id=1, replica_groups=mesh['leaf'=8,'rows'=4] {'leaf'}, dimensions={0} | all-to-all | bytes 12288 | tf_op jit(solution)/shard_map/all_to_all | solution.py:66
  82.0 3.2 %scatter_custom_fusion.1 = f32[8,1024]{0,1:T(8,128)S(1)} fusion(s32[1024]{0:T(1024)S(1)} %get-tuple-element.14, f32[1024,8]{1,0:T(8,128)S(1)} %copy.194, f32[]{:T(128)} %constant.15.clone.1), kind=kCustom, calls=%fused_computation.52 | custom fusion | bytes 32772 | tf_op jit(solution)/shard_map/scatter | solution.py:78
  85.6 5.8 %psum.71 = f32[8]{0:T(128)S(1)} all-reduce(f32[8]{0:T(128)S(1)} %get-tuple-element.12), channel_id=1, replica_groups=mesh['leaf'=8,'rows'=4] {'rows'}, use_global_device_ids=true, to_apply=%region_3.5 | all-reduce | flops 8 | bytes 64 | tf_op jit(solution)/shard_map/psum | solution.py:10
  91.4 38.2 %psum.74 = f32[8]{0:T(128)S(1)} all-reduce(f32[8]{0:T(128)S(1)} %get-tuple-element.11), channel_id=1, replica_groups=mesh['leaf'=8,'rows'=4] {'leaf','rows'}, use_global_device_ids=true, to_apply=%region_8.10 | all-reduce | flops 8 | bytes 64 | tf_op jit(solution)/shard_map/psum | solution.py:15
  129.5 20.4 %psum.72 = f32[8]{0:T(128)S(1)} all-reduce(f32[8]{0:T(128)S(1)} %psum.71), channel_id=1, replica_groups=mesh['leaf'=8,'rows'=4] {'leaf'}, use_global_device_ids=true, to_apply=%region_4.6 | all-reduce | flops 8 | bytes 64 | tf_op jit(solution)/shard_map/psum | solution.py:11
  150.2 3.2 %gather_fusion.2 = bf16[1024,8]{1,0:T(8,128)(2,1)S(1)} fusion(bf16[8,1024]{0,1:T(8,128)(2,1)S(1)} %copy.196, s32[1024]{0:T(1024)S(1)} %broadcast_clamp_fusion), kind=kCustom, calls=%fused_computation.2.clone | custom fusion | bytes 36864 | tf_op jit(solution)/shard_map/jit(_take)/gather | solution.py:37
  153.6 0.5 fusion.4
  154.4 0.7 reduce.12
  155.1 8.9 %all_to_all.82 = bf16[8,2,192]{2,1,0:T(2,128)(2,1)S(1)} all-to-all(bf16[8,2,192]{2,1,0:T(2,128)(2,1)S(1)} %reshape.254), channel_id=1, replica_groups=mesh['leaf'=8,'rows'=4] {'leaf'}, dimensions={0} | all-to-all | bytes 12288 | tf_op jit(solution)/shard_map/all_to_all | solution.py:44
  164.4 6.1 %psum.75 = bf16[8,192]{1,0:T(8,128)(2,1)S(1)} all-reduce(f32[8,192]{1,0:T(8,128)S(1)} %convolution_bitcast_fusion.5), channel_id=1, replica_groups=mesh['leaf'=8,'rows'=4] {'rows'}, use_global_device_ids=true, to_apply=%region_9.11 | all-reduce | flops 1536 | bytes 9216 | tf_op jit(solution)/shard_map/psum | solution.py:56
  171.2 0.7 reduce.13
  172.0 8.9 %all_to_all.83 = bf16[8,2,192]{2,1,0:T(2,128)(2,1)S(1)} all-to-all(bf16[8,2,192]{2,1,0:T(2,128)(2,1)S(1)} %reshape.256), channel_id=1, replica_groups=mesh['leaf'=8,'rows'=4] {'leaf'}, dimensions={0} | all-to-all | bytes 12288 | tf_op jit(solution)/shard_map/all_to_all | solution.py:66
  181.7 3.2 %scatter_custom_fusion.2 = f32[8,1024]{0,1:T(8,128)S(1)} fusion(s32[1024]{0:T(1024)S(1)} %get-tuple-element.14, f32[1024,8]{1,0:T(8,128)S(1)} %copy.207, f32[]{:T(128)} %constant.15.clone.1), kind=kCustom, calls=%fused_computation.50 | custom fusion | bytes 32772 | tf_op jit(solution)/shard_map/scatter | solution.py:78
  185.2 5.8 %psum.76 = f32[8]{0:T(128)S(1)} all-reduce(f32[8]{0:T(128)S(1)} %multiply_reduce_fusion.1), channel_id=1, replica_groups=mesh['leaf'=8,'rows'=4] {'rows'}, use_global_device_ids=true, to_apply=%region_12.14 | all-reduce | flops 8 | bytes 64 | tf_op jit(solution)/shard_map/psum | solution.py:10
  190.9 17.7 %psum.77 = f32[8]{0:T(128)S(1)} all-reduce(f32[8]{0:T(128)S(1)} %psum.76), channel_id=1, replica_groups=mesh['leaf'=8,'rows'=4] {'leaf'}, use_global_device_ids=true, to_apply=%region_13.15 | all-reduce | flops 8 | bytes 64 | tf_op jit(solution)/shard_map/psum | solution.py:11
  208.9 3.2 %gather_fusion.3 = bf16[1024,8]{1,0:T(8,128)(2,1)S(1)} fusion(bf16[8,1024]{0,1:T(8,128)(2,1)S(1)} %copy.209, s32[1024]{0:T(1024)S(1)} %broadcast_clamp_fusion), kind=kCustom, calls=%fused_computation.3.clone | custom fusion | bytes 36864 | tf_op jit(solution)/shard_map/jit(_take)/gather | solution.py:37
  212.2 0.5 fusion.6
  213.0 0.7 reduce.14
  213.8 9.0 %all_to_all.84 = bf16[8,2,192]{2,1,0:T(2,128)(2,1)S(1)} all-to-all(bf16[8,2,192]{2,1,0:T(2,128)(2,1)S(1)} %reshape.258), channel_id=1, replica_groups=mesh['leaf'=8,'rows'=4] {'leaf'}, dimensions={0} | all-to-all | bytes 12288 | tf_op jit(solution)/shard_map/all_to_all | solution.py:44
  223.2 5.8 %psum.78 = bf16[8,192]{1,0:T(8,128)(2,1)S(1)} all-reduce(f32[8,192]{1,0:T(8,128)S(1)} %convolution_bitcast_fusion.4), channel_id=1, replica_groups=mesh['leaf'=8,'rows'=4] {'rows'}, use_global_device_ids=true, to_apply=%region_14.16 | all-reduce | flops 1536 | bytes 9216 | tf_op jit(solution)/shard_map/psum | solution.py:56
  229.7 0.7 reduce.15
  230.5 8.9 %all_to_all.85 = bf16[8,2,192]{2,1,0:T(2,128)(2,1)S(1)} all-to-all(bf16[8,2,192]{2,1,0:T(2,128)(2,1)S(1)} %reshape.260), channel_id=1, replica_groups=mesh['leaf'=8,'rows'=4] {'leaf'}, dimensions={0} | all-to-all | bytes 12288 | tf_op jit(solution)/shard_map/all_to_all | solution.py:66
  240.2 3.2 %scatter_custom_fusion.3 = f32[8,1024]{0,1:T(8,128)S(1)} fusion(s32[1024]{0:T(1024)S(1)} %get-tuple-element.14, f32[1024,8]{1,0:T(8,128)S(1)} %copy.220, f32[]{:T(128)} %constant.15.clone.1), kind=kCustom, calls=%fused_computation.48 | custom fusion | bytes 32772 | tf_op jit(solution)/shard_map/scatter | solution.py:78
  243.7 38.2 %psum.79 = f32[8]{0:T(128)S(1)} all-reduce(f32[8]{0:T(128)S(1)} %multiply_reduce_fusion), channel_id=1, replica_groups=mesh['leaf'=8,'rows'=4] {'leaf','rows'}, use_global_device_ids=true, to_apply=%region_17.19 | all-reduce | flops 8 | bytes 64 | tf_op jit(solution)/shard_map/psum | solution.py:15
  281.9 0.7 multiply_subtract_fusion
  (118 shorter events, 12.5 us)
Async XLA Ops:
  0.6 16.6 %copy-start = (bf16[48,1024]{1,0:T(8,128)(2,1)S(1)}, bf16[48,1024]{1,0:T(8,128)(2,1)}, u32[]{:S(2)}) copy-start(bf16[48,1024]{1,0:T(8,128)(2,1)} %param.17) | copy-start | bytes 294916
  7.1 0.7 copy-start.5
  7.9 9.4 %copy-start.3 = (bf16[384,192]{0,1:T(8,128)(2,1)S(1)}, bf16[384,192]{0,1:T(8,128)(2,1)}, u32[]{:S(2)}) copy-start(bf16[384,192]{0,1:T(8,128)(2,1)} %param.16) | copy-start | bytes 442372
  9.9 13.8 %all-to-all-start = ((bf16[8,2,192]{2,1,0:T(2,128)(2,1)}), bf16[8,2,192]{2,1,0:T(2,128)(2,1)S(1)}, u32[]{:S(2)}, u32[]{:S(2)}) async-start(bf16[8,2,192]{2,1,0:T(2,128)(2,1)} %reshape.246), calls=%async_computation | async-start | bytes 16384 | tf_op jit(solution)/shard_map/all_to_all | solution.py:44
  48.3 0.8 copy-start.1
  48.3 0.8 copy-start.2
  52.5 5.5 %copy-start.4 = (bf16[384,192]{0,1:T(8,128)(2,1)S(1)}, bf16[384,192]{0,1:T(8,128)(2,1)}, u32[]{:S(2)}) copy-start(bf16[384,192]{0,1:T(8,128)(2,1)} %param.15) | copy-start | bytes 442372
  54.7 9.8 %all-to-all-start.2 = ((bf16[8,2,192]{2,1,0:T(2,128)(2,1)}), bf16[8,2,192]{2,1,0:T(2,128)(2,1)S(1)}, u32[]{:S(2)}, u32[]{:S(2)}) async-start(bf16[8,2,192]{2,1,0:T(2,128)(2,1)} %reshape.250), calls=%async_computation.2 | async-start | bytes 16384 | tf_op jit(solution)/shard_map/all_to_all | solution.py:44
